TPU v7x, 32 devices: a whole 2x2x4 slice. The times are simulated.
32 devices in a mesh: groups: 2 (over x), dp: 2 (over core), seq: 8 (over z, y).
Axes of the slice: x: 2, y: 2, z: 4, core: 2. Of those that a mesh axis runs over, the one named last changes fastest.
Arguments:
- history: bfloat16 [8, 768, 1024], P(('groups', 'dp'), 'seq'), parts along dimension 0, may hold values from -20 to 20
- candidates: bfloat16 [4, 512, 1024], P(('groups', 'dp'), 'seq'), parts along dimension 0, may hold values from -6 to 6
- lengths: int32 [8], P(('groups', 'dp')), parts along dimension 0, may hold values from 96 to 768
- assignment: int32 [4, 512], P(('groups', 'dp'), 'seq'), parts along dimension 0, may hold values from 0 to 1, as said below
- weight_in: bfloat16 [1024, 4096], replicated, may hold values from -0.1875 to 0.1875
- weight_out: bfloat16 [1024, 1024], replicated, may hold values from -0.1875 to 0.1875
- gain_in: float32 [1024], replicated, may hold values from 0.25 to 1.75
- gain_attn: float32 [1024], replicated, may hold values from 0.25 to 1.75
Outputs:
- history_out: bfloat16 [8, 768, 1024], P(('groups', 'dp'), 'seq'), parts along dimension 0
- candidate_out: bfloat16 [4, 512, 1024], P(('groups', 'dp'), 'seq'), parts along dimension 0
There are 2 independent parts, one for each index of `groups`. A program takes and returns all parts, laid end to end along the dimension named above; an argument that names none is the same for every part. Nothing has to cross between parts.
Inputs may be any that keep to these rules, and one draw needn't show every extreme that they name: `assignment`: of the 64 candidates of one device, at most 40 belong to either history; in every dp index some device has exactly 40 of the first and another exactly 40 of the second.
All inputs are finite; a program needn't handle non-finite values.
Results may differ from a plain program's by a relative error of at most 0.0075.
Values may be sent and summed in bfloat16 or wider, within the bound.
A program may use at most 192 MiB of HBM per device.

v0:
```python
import math
import jax
import jax.numpy as jnp
from jax import lax
from jax.sharding import PartitionSpec as P

H = 16
HD = 64
CAP = 40


def rms_apply(values, gain):
    return values * lax.rsqrt(jnp.mean(values * values, axis=-1, keepdims=True) + 1e-06) * gain


def self_item(packed):
    query, keys, values, valid = packed
    length = keys.shape[0]
    score_scale = HD ** (-0.5)
    block_rows = math.gcd(length, 512)
    key_positions = jnp.arange(length, dtype=jnp.int32)

    def query_part(inner):
        query_block, first_row = inner
        scores = jnp.dot(query_block, keys.T, preferred_element_type=jnp.float32) * score_scale
        row_positions = first_row + jnp.arange(block_rows, dtype=jnp.int32)
        allowed = (key_positions[None, :] <= row_positions[:, None]) & (
            key_positions[None, :] < valid
        )
        weights = jnp.where(allowed, jax.nn.silu(scores), 0.0).astype(jnp.bfloat16)
        return jnp.dot(weights, values, preferred_element_type=jnp.float32).astype(jnp.bfloat16)

    starts = jnp.arange(length // block_rows, dtype=jnp.int32) * block_rows
    result = lax.map(query_part, (query.reshape(length // block_rows, block_rows, HD), starts))
    return result.reshape(length, HD)


def cand_item(packed):
    queries, keys, values, valid = packed
    cand_total = queries.shape[0]
    score_scale = HD ** (-0.5)
    block_rows = math.gcd(cand_total, 1024)
    key_positions = jnp.arange(keys.shape[0], dtype=jnp.int32)

    def cand_part(query_block):
        scores = jnp.dot(query_block, keys.T, preferred_element_type=jnp.float32) * score_scale
        weights = jnp.where(key_positions[None, :] < valid, jax.nn.silu(scores), 0.0).astype(
            jnp.bfloat16
        )
        return jnp.dot(weights, values, preferred_element_type=jnp.float32).astype(jnp.bfloat16)

    result = lax.map(cand_part, queries.reshape(cand_total // block_rows, block_rows, HD))
    return result.reshape(cand_total, HD)


def place_windows(windows, cand_count, window_rows, inverse):
    first = jnp.pad(windows[0], ((0, cand_count - window_rows), (0, 0), (0, 0)))
    second = jnp.pad(windows[1], ((cand_count - window_rows, 0), (0, 0), (0, 0)))
    return (first + second)[inverse]


def per_device(history, candidates, lengths, assignment, weight_in, weight_out, gain_in, gain_attn):
    seq_devices = lax.axis_size("seq")
    hist_local, tok_share, model_width = history.shape
    item_count = hist_local * H
    items_local = item_count // seq_devices
    length = tok_share * seq_devices
    hist_float = history.astype(jnp.float32)
    normed = (
        rms_apply(hist_float, gain_in)
        .astype(jnp.bfloat16)
        .reshape(hist_local * tok_share, model_width)
    )
    projected = jnp.dot(normed, weight_in, preferred_element_type=jnp.float32)
    gate = jax.nn.silu(projected[:, :model_width]).astype(jnp.bfloat16)
    query = projected[:, model_width : 2 * model_width].astype(jnp.bfloat16)
    keys = projected[:, 2 * model_width : 3 * model_width].astype(jnp.bfloat16)
    values = projected[:, 3 * model_width :].astype(jnp.bfloat16)

    def to_items(matrix):
        return (
            matrix.reshape(hist_local, tok_share, H, HD)
            .transpose(0, 2, 1, 3)
            .reshape(item_count, tok_share * HD)
        )

    exchanged = (
        lax.all_to_all(to_items(query), "seq", split_axis=0, concat_axis=1, tiled=True),
        lax.all_to_all(to_items(keys), "seq", split_axis=0, concat_axis=1, tiled=True),
        lax.all_to_all(to_items(values), "seq", split_axis=0, concat_axis=1, tiled=True),
    )
    heads_query = exchanged[0].reshape(items_local, length, HD)
    heads_keys = exchanged[1].reshape(items_local, length, HD)
    heads_values = exchanged[2].reshape(items_local, length, HD)
    first_item = lax.axis_index("seq") * items_local
    item_hist = (first_item + jnp.arange(items_local, dtype=jnp.int32)) // H
    members = jnp.arange(hist_local, dtype=jnp.int32)
    item_valid = jnp.sum(
        jnp.where(item_hist[:, None] == members[None, :], lengths[None, :], 0), axis=1
    )
    attended = lax.map(self_item, (heads_query, heads_keys, heads_values, item_valid))
    returned = lax.all_to_all(
        attended.reshape(items_local, length * HD), "seq", split_axis=1, concat_axis=0, tiled=True
    )
    returned = (
        returned.reshape(hist_local, H, tok_share, HD)
        .transpose(0, 2, 1, 3)
        .reshape(hist_local * tok_share, model_width)
    )
    gated_rows = (
        rms_apply(returned.astype(jnp.float32), gain_attn) * gate.astype(jnp.float32)
    ).astype(jnp.bfloat16)
    history_out = hist_float.reshape(hist_local * tok_share, model_width) + jnp.dot(
        gated_rows, weight_out, preferred_element_type=jnp.float32
    )
    history_out = history_out.astype(jnp.bfloat16).reshape(hist_local, tok_share, model_width)
    cand_rows = candidates[0]
    cand_count = cand_rows.shape[0]
    window_rows = CAP
    owner = assignment[0]
    cand_float = cand_rows.astype(jnp.float32)
    cand_normed = rms_apply(cand_float, gain_in).astype(jnp.bfloat16)
    cand_proj = jnp.dot(
        cand_normed, weight_in[:, : 2 * model_width], preferred_element_type=jnp.float32
    )
    cand_gate = jax.nn.silu(cand_proj[:, :model_width]).astype(jnp.bfloat16)
    cand_query = cand_proj[:, model_width:].astype(jnp.bfloat16).reshape(cand_count, H, HD)
    order = jnp.argsort(owner * cand_count + jnp.arange(cand_count, dtype=jnp.int32))
    inverse = jnp.argsort(order)
    sorted_query = cand_query[order]
    sorted_owner = owner[order]
    window_starts = [0, cand_count - window_rows]
    window_list = []
    for member in range(hist_local):
        start = window_starts[member]
        rows_here = sorted_query[start : start + window_rows]
        mine = sorted_owner[start : start + window_rows] == member
        window_list.append(jnp.where(mine[:, None, None], rows_here, jnp.zeros_like(rows_here)))
    window_query = jnp.stack(window_list)
    outgoing = window_query.transpose(0, 2, 1, 3).reshape(item_count, window_rows * HD)
    incoming = lax.all_to_all(outgoing, "seq", split_axis=0, concat_axis=1, tiled=True)
    incoming = incoming.reshape(items_local, seq_devices * window_rows, HD)
    results = lax.map(cand_item, (incoming, heads_keys, heads_values, item_valid))
    back_home = lax.all_to_all(
        results.reshape(items_local, seq_devices * window_rows * HD),
        "seq",
        split_axis=1,
        concat_axis=0,
        tiled=True,
    )
    back_home = (
        back_home.reshape(hist_local, H, window_rows, HD).transpose(0, 2, 1, 3).astype(jnp.float32)
    )
    cross_attended = (
        place_windows(back_home, cand_count, window_rows, inverse)
        .astype(jnp.bfloat16)
        .reshape(cand_count, model_width)
    )
    cand_gated = (
        rms_apply(cross_attended.astype(jnp.float32), gain_attn) * cand_gate.astype(jnp.float32)
    ).astype(jnp.bfloat16)
    candidate_out = (
        cand_float + jnp.dot(cand_gated, weight_out, preferred_element_type=jnp.float32)
    ).astype(jnp.bfloat16)
    return (history_out, candidate_out[None])


def solution(mesh):
    in_specs = (
        P(("groups", "dp"), "seq", None),
        P(("groups", "dp"), "seq", None),
        P(("groups", "dp")),
        P(("groups", "dp"), "seq"),
        P(),
        P(),
        P(),
        P(),
    )
    out_specs = (P(("groups", "dp"), "seq", None), P(("groups", "dp"), "seq", None))
    return jax.shard_map(
        per_device, mesh=mesh, in_specs=in_specs, out_specs=out_specs, check_vma=False
    )
```

profile of v0, /device:TPU:0, one launch (start us, length us, event | category | flops | bytes accessed | tf_op | source)
XLA Modules:
  0.0 198.5 jit_solution(17433720871256379200)
XLA Ops:
  1.5 2.0 %sort.31 = (s32[64]{0:T(128)}, s32[64]{0:T(128)S(1)}) sort(s32[64]{0:T(128)S(1)} %iota_add_fusion.1, s32[64]{0:T(128)S(1)} %iota.37), dimensions={0}, to_apply=%region_8.9 | sort | flops 384 | bytes 1024 | tf_op jit(solution)/shard_map/jit(argsort)/sort | solution.py:128
  3.5 1.0 fusion.46
  4.6 3.2 %fusion.37 = f32[64,2048]{1,0:T(8,128)S(1)} fusion(bf16[1024,4096]{1,0:T(8,128)(2,1)} %param.20, bf16[1,64,1024]{2,1,0:T(8,128)(2,1)} %param.17, f32[1024]{0:T(1024)} %param.22, f32[64]{0:T(128)S(1)} %add_rsqrt_fusion.3), kind=kOutput, calls=%fused_computation.50 | convolution fusion | flops 268697600 | bytes 4854016 | tf_op jit(solution)/shard_map/dot_general | solution.py:123
  11.5 7.3 %all-to-all-start.4 = ((bf16[8,4,2560]{2,1,0:T(4,128)(2,1)}), bf16[8,4,2560]{2,1,0:T(4,128)(2,1)}, u32[]{:S(2)}, u32[]{:S(2)}) async-start(bf16[8,4,2560]{2,1,0:T(4,128)(2,1)} %all_to_all.79), calls=%async_computation.4 | async-start | bytes 327680 | tf_op jit(solution)/shard_map/all_to_all | solution.py:141
  19.1 6.9 %fusion.62 = (bf16[192,4096]{1,0:T(8,128)(2,1)S(1)}, f32[192,4096]{1,0:T(8,128)}) fusion(bf16[192,1024]{1,0:T(8,128)(2,1)S(1)} %bitcast.139, bf16[1024,4096]{1,0:T(8,128)(2,1)} %param.20), kind=kOutput, calls=%fused_computation.113 | convolution fusion | flops 1611399168 | bytes 13500416 | tf_op jit(solution)/shard_map/dot_general | solution.py:74
  26.0 1.0 fusion.61
  28.1 1.3 all_to_all.71
  29.4 6.0 %all-to-all-start.1 = ((bf16[8,4,6144]{2,1,0:T(4,128)(2,1)}), bf16[8,4,6144]{2,1,0:T(4,128)(2,1)}, u32[]{:S(2)}, u32[]{:S(2)}) async-start(bf16[8,4,6144]{2,1,0:T(4,128)(2,1)} %all_to_all.71), calls=%async_computation.1 | async-start | bytes 786432 | tf_op jit(solution)/shard_map/all_to_all | solution.py:89
  35.3 1.2 copy.68
  37.4 1.3 all_to_all.74
  38.7 7.8 %all-to-all-done.1 = bf16[8,4,6144]{2,1,0:T(4,128)(2,1)} async-done(((bf16[8,4,6144]{2,1,0:T(4,128)(2,1)}), bf16[8,4,6144]{2,1,0:T(4,128)(2,1)}, u32[]{:S(2)}, u32[]{:S(2)}) %all-to-all-start.1) | async-done | bytes 393248 | tf_op jit(solution)/shard_map/all_to_all | solution.py:89
  46.6 4.1 %all-to-all-start.2 = ((bf16[8,4,6144]{2,1,0:T(4,128)(2,1)}), bf16[8,4,6144]{2,1,0:T(4,128)(2,1)}, u32[]{:S(2)}, u32[]{:S(2)}) async-start(bf16[8,4,6144]{2,1,0:T(4,128)(2,1)} %all_to_all.74), calls=%async_computation.2 | async-start | bytes 786432 | tf_op jit(solution)/shard_map/all_to_all | solution.py:90
  50.7 2.0 %sort.32 = (s32[64]{0:T(128)}, s32[64]{0:T(128)S(1)}) sort(s32[64]{0:T(128)S(1)} %get-tuple-element.151, s32[64]{0:T(128)S(1)} %iota.38), dimensions={0}, to_apply=%region_14.15 | sort | flops 384 | bytes 1024 | tf_op jit(solution)/shard_map/jit(argsort)/sort | solution.py:129
  52.7 1.2 copy.62
  54.8 1.3 all_to_all.68
  58.1 1.2 copy.67
  60.1 1.7 all-to-all-done.2
  61.9 4.2 %all-to-all-start = ((bf16[8,4,6144]{2,1,0:T(4,128)(2,1)}), bf16[8,4,6144]{2,1,0:T(4,128)(2,1)}, u32[]{:S(2)}, u32[]{:S(2)}) async-start(bf16[8,4,6144]{2,1,0:T(4,128)(2,1)} %all_to_all.68), calls=%async_computation | async-start | bytes 786432 | tf_op jit(solution)/shard_map/all_to_all | solution.py:88
  66.0 1.2 copy.70
  67.3 1.7 reshape.190
  68.9 32.8 %while.46 = (s32[]{:T(128)}, bf16[4,320,64]{2,1,0:T(8,128)(2,1)}, bf16[4,320,64]{2,1,0:T(8,128)(2,1)}, bf16[4,768,64]{2,1,0:T(8,128)(2,1)S(1)}, s32[4]{0:T(128)S...) while((s32[]{:T(128)}, bf16[4,320,64]{2,1,0:T(8,128)(2,1)}, ...), condition=%wide.region_13.14_spmd, body=%wide.region_10.13_spmd.sunk | while | flops 12931844 | bytes 1027586 | solution.py:143
  68.9 1.0 dynamic-slice_bitcast_fusion.7
  71.4 5.1 %while.48 = (s32[]{:T(128)}, bf16[5,64,64]{2,1,0:T(8,128)(2,1)S(1)}, s32[]{:T(128)}, bf16[5,64,64]{2,1,0:T(8,128)(2,1)S(1)}, bf16[768,64]{1,0:T(8,128)(2,1)S(1)}, /*index=5*/bf16[768,64]{1,0:T(8,128)(2,1)S(1)}, s32[]{:T(128)}) while((s32[]{:T(128)}, bf16[5,64,64]{2,1,0:T(8,128)(2,1)S(1)}, s32[]{:T(128)}, ...), condition=%wide.region_12.12_spmd.clone, body=%wide.region_11.11_spmd.clone.sunk | while | flops 12931842 | bytes 428881 | solution.py:52
  77.1 1.0 dynamic-slice_bitcast_fusion.7
  79.6 5.1 %while.48 = (s32[]{:T(128)}, bf16[5,64,64]{2,1,0:T(8,128)(2,1)S(1)}, s32[]{:T(128)}, bf16[5,64,64]{2,1,0:T(8,128)(2,1)S(1)}, bf16[768,64]{1,0:T(8,128)(2,1)S(1)}, /*index=5*/bf16[768,64]{1,0:T(8,128)(2,1)S(1)}, s32[]{:T(128)}) while((s32[]{:T(128)}, bf16[5,64,64]{2,1,0:T(8,128)(2,1)S(1)}, s32[]{:T(128)}, ...), condition=%wide.region_12.12_spmd.clone, body=%wide.region_11.11_spmd.clone.sunk | while | flops 12931842 | bytes 428881 | solution.py:52
  85.3 1.0 dynamic-slice_bitcast_fusion.7
  87.8 5.1 %while.48 = (s32[]{:T(128)}, bf16[5,64,64]{2,1,0:T(8,128)(2,1)S(1)}, s32[]{:T(128)}, bf16[5,64,64]{2,1,0:T(8,128)(2,1)S(1)}, bf16[768,64]{1,0:T(8,128)(2,1)S(1)}, /*index=5*/bf16[768,64]{1,0:T(8,128)(2,1)S(1)}, s32[]{:T(128)}) while((s32[]{:T(128)}, bf16[5,64,64]{2,1,0:T(8,128)(2,1)S(1)}, s32[]{:T(128)}, ...), condition=%wide.region_12.12_spmd.clone, body=%wide.region_11.11_spmd.clone.sunk | while | flops 12931842 | bytes 428881 | solution.py:52
  93.5 1.0 dynamic-slice_bitcast_fusion.7
  96.0 5.1 %while.48 = (s32[]{:T(128)}, bf16[5,64,64]{2,1,0:T(8,128)(2,1)S(1)}, s32[]{:T(128)}, bf16[5,64,64]{2,1,0:T(8,128)(2,1)S(1)}, bf16[768,64]{1,0:T(8,128)(2,1)S(1)}, /*index=5*/bf16[768,64]{1,0:T(8,128)(2,1)S(1)}, s32[]{:T(128)}) while((s32[]{:T(128)}, bf16[5,64,64]{2,1,0:T(8,128)(2,1)S(1)}, s32[]{:T(128)}, ...), condition=%wide.region_12.12_spmd.clone, body=%wide.region_11.11_spmd.clone.sunk | while | flops 12931842 | bytes 428881 | solution.py:52
  101.7 1.2 all_to_all.82
  103.7 6.0 %all-to-all-start.5 = ((bf16[4,8,2560]{2,0,1:T(4,128)(2,1)}), bf16[4,8,2560]{2,0,1:T(4,128)(2,1)}, u32[]{:S(2)}, u32[]{:S(2)}) async-start(bf16[4,8,2560]{2,0,1:T(4,128)(2,1)} %copy.76), calls=%async_computation.5 | async-start | bytes 327680 | tf_op jit(solution)/shard_map/all_to_all | solution.py:144
  109.7 1.2 copy.64
  110.9 1.7 reshape.186
  112.6 55.4 %while.44 = (s32[]{:T(128)}, bf16[4,768,64]{2,1,0:T(8,128)(2,1)}, bf16[4,768,64]{2,1,0:T(8,128)(2,1)}, bf16[4,768,64]{2,1,0:T(8,128)(2,1)S(1)}, s32[4]{0:T(128)S...) while((s32[]{:T(128)}, bf16[4,768,64]{2,1,0:T(8,128)(2,1)}, ...), condition=%wide.region_5.6_spmd, body=%wide.region_2.5_spmd.sunk | while | flops 52118532 | bytes 1578542 | solution.py:101
  112.6 1.0 dynamic-slice_bitcast_fusion.6
  115.1 9.6 %while.47 = (s32[]{:T(128)}, bf16[3,256,64]{1,2,0:T(8,128)(2,1)}, s32[3]{0:T(128)S(1)}, s32[]{:T(128)}, bf16[3,256,64]{2,1,0:T(8,128)(2,1)S(1)}, /*index=5*/bf16...) while((s32[]{:T(128)}, bf16[3,256,64]{1,2,0:T(8,128)(2,1)}, ...), condition=%wide.region_4.4_spmd.clone.clone, body=%wide.region_3.3_spmd.clone.clone.sunk | while | flops 52118528 | bytes 496489 | solution.py:34
  117.0 1.3 fusion.86
  120.2 1.3 fusion.86
  123.4 1.3 fusion.86
  124.7 1.1 copy.83
  128.9 9.6 %while.47 = (s32[]{:T(128)}, bf16[3,256,64]{1,2,0:T(8,128)(2,1)}, s32[3]{0:T(128)S(1)}, s32[]{:T(128)}, bf16[3,256,64]{2,1,0:T(8,128)(2,1)S(1)}, /*index=5*/bf16...) while((s32[]{:T(128)}, bf16[3,256,64]{1,2,0:T(8,128)(2,1)}, ...), condition=%wide.region_4.4_spmd.clone.clone, body=%wide.region_3.3_spmd.clone.clone.sunk | while | flops 52118528 | bytes 496489 | solution.py:34
  130.9 1.3 fusion.86
  134.1 1.3 fusion.86
  137.3 1.3 fusion.86
  138.6 1.1 copy.83
  142.8 9.6 %while.47 = (s32[]{:T(128)}, bf16[3,256,64]{1,2,0:T(8,128)(2,1)}, s32[3]{0:T(128)S(1)}, s32[]{:T(128)}, bf16[3,256,64]{2,1,0:T(8,128)(2,1)S(1)}, /*index=5*/bf16...) while((s32[]{:T(128)}, bf16[3,256,64]{1,2,0:T(8,128)(2,1)}, ...), condition=%wide.region_4.4_spmd.clone.clone, body=%wide.region_3.3_spmd.clone.clone.sunk | while | flops 52118528 | bytes 496489 | solution.py:34
  144.7 1.3 fusion.86
  147.9 1.3 fusion.86
  151.1 1.3 fusion.86
  152.4 1.1 copy.83
  156.6 9.6 %while.47 = (s32[]{:T(128)}, bf16[3,256,64]{1,2,0:T(8,128)(2,1)}, s32[3]{0:T(128)S(1)}, s32[]{:T(128)}, bf16[3,256,64]{2,1,0:T(8,128)(2,1)S(1)}, /*index=5*/bf16...) while((s32[]{:T(128)}, bf16[3,256,64]{1,2,0:T(8,128)(2,1)}, ...), condition=%wide.region_4.4_spmd.clone.clone, body=%wide.region_3.3_spmd.clone.clone.sunk | while | flops 52118528 | bytes 496489 | solution.py:34
  158.6 1.3 fusion.86
  161.8 1.3 fusion.86
  165.0 1.3 fusion.86
  166.3 1.1 copy.83
  168.0 1.8 all_to_all.77
  169.8 1.1 copy.71
  170.8 6.0 %all-to-all-start.3 = ((bf16[4,8,6144]{2,0,1:T(4,128)(2,1)}), bf16[4,8,6144]{2,0,1:T(4,128)(2,1)S(1)}, u32[]{:S(2)}, u32[]{:S(2)}) async-start(bf16[4,8,6144]{2,0,1:T(4,128)(2,1)} %copy.71), calls=%async_computation.3 | async-start | bytes 786432 | tf_op jit(solution)/shard_map/all_to_all | solution.py:102
  179.7 2.1 %fusion.41 = bf16[1,64,1024]{2,1,0:T(8,128)(2,1)} fusion(bf16[1024,1024]{1,0:T(8,128)(2,1)S(1)} %copy-done, f32[64,1024]{1,0:T(8,128)S(1)} %reshape.196, f32[64,2048]{1,0:T(8,128)} %copy-done.5, bf16[1,64,1024]{2,1,0:T(8,128)(2,1)S(1)} %copy-done.4, f32[1024]{0:T(1024)S(1)} %copy-done.7, f32[64]{0:T(128)S(1)} %add_rsqrt_fusion.2), kind=kOutput, calls=%fused_computation.56 | convolution fusion | flops 135069696 | bytes 2887936 | tf_op jit(solution)/shard_map/dot_general | solution.py:163
  181.8 4.8 %all-to-all-done.3 = bf16[4,8,6144]{2,0,1:T(4,128)(2,1)S(1)} async-done(((bf16[4,8,6144]{2,0,1:T(4,128)(2,1)}), bf16[4,8,6144]{2,0,1:T(4,128)(2,1)S(1)}, u32[]{:S(2)}, u32[]{:S(2)}) %all-to-all-start.3) | async-done | bytes 393248 | tf_op jit(solution)/shard_map/all_to_all | solution.py:102
  186.7 1.9 reshape.198
  188.6 3.5 %copy.78 = f32[2,96,16,64]{3,2,1,0:T(8,128)} copy(f32[2,96,16,64]{3,1,2,0:T(8,128)} %bitcast.136) | data formatting | bytes 1572864 | tf_op jit(solution)/shard_map/convert_element_type | solution.py:111
  192.1 2.7 %reshape.226 = f32[192,1024]{1,0:T(8,128)} reshape(f32[2,96,16,64]{3,2,1,0:T(8,128)} %copy.78) | data formatting | bytes 1572864 | tf_op jit(solution)/shard_map/convert_element_type | solution.py:111
  195.7 2.8 %fusion.39 = bf16[192,1024]{1,0:T(8,128)(2,1)} fusion(bf16[1024,1024]{1,0:T(8,128)(2,1)S(1)} %copy-done, f32[192,1024]{1,0:T(8,128)} %reshape.226, f32[192,4096]{1,0:T(8,128)} %get-tuple-element.268, f32[1024]{0:T(1024)S(1)} %copy-done.7, f32[192]{0:T(256)S(1)} %rsqrt.37, bf16[192,1024]{1,0:T(8,128)(2,1)S(1)} %bitcast.145), kind=kOutput, calls=%fused_computation.53 | convolution fusion | flops 405209088 | bytes 4461312 | tf_op jit(solution)/shard_map/dot_general | solution.py:113
  (186 shorter events, 78.2 us)
Async XLA Ops:
  0.6 179.1 %copy-start = (bf16[1024,1024]{1,0:T(8,128)(2,1)S(1)}, bf16[1024,1024]{1,0:T(8,128)(2,1)}, u32[]{:S(2)}) copy-start(bf16[1024,1024]{1,0:T(8,128)(2,1)} %param.21) | copy-start | bytes 6291460
  4.5 4.9 %copy-start.1 = (s32[1,64]{1,0:T(1,128)S(1)}, s32[1,64]{1,0:T(1,128)}, u32[]{:S(2)}) copy-start(s32[1,64]{1,0:T(1,128)} %param.19) | copy-start | bytes 772
  7.8 0.8 copy-start.5
  8.6 10.2 %copy-start.2 = (bf16[2,96,1024]{2,1,0:T(8,128)(2,1)S(1)}, bf16[2,96,1024]{2,1,0:T(8,128)(2,1)}, u32[]{:S(2)}) copy-start(bf16[2,96,1024]{2,1,0:T(8,128)(2,1)} %param.16) | copy-start | bytes 1179652
  8.6 10.4 %copy-start.6 = (f32[1024]{0:T(1024)S(1)}, f32[1024]{0:T(1024)}, u32[]{:S(2)}) copy-start(f32[1024]{0:T(1024)} %param.22) | copy-start | bytes 12292
  11.5 17.9 %all-to-all-start.4 = ((bf16[8,4,2560]{2,1,0:T(4,128)(2,1)}), bf16[8,4,2560]{2,1,0:T(4,128)(2,1)}, u32[]{:S(2)}, u32[]{:S(2)}) async-start(bf16[8,4,2560]{2,1,0:T(4,128)(2,1)} %all_to_all.79), calls=%async_computation.4 | async-start | bytes 327680 | tf_op jit(solution)/shard_map/all_to_all | solution.py:141
  29.4 17.2 %all-to-all-start.1 = ((bf16[8,4,6144]{2,1,0:T(4,128)(2,1)}), bf16[8,4,6144]{2,1,0:T(4,128)(2,1)}, u32[]{:S(2)}, u32[]{:S(2)}) async-start(bf16[8,4,6144]{2,1,0:T(4,128)(2,1)} %all_to_all.71), calls=%async_computation.1 | async-start | bytes 786432 | tf_op jit(solution)/shard_map/all_to_all | solution.py:89
  37.4 18.7 %copy-start.8 = (s32[2]{0:T(128)S(1)}, s32[2]{0:T(128)}, u32[]{:S(2)}) copy-start(s32[2]{0:T(128)} %param.18) | copy-start | bytes 28
  46.6 15.3 %all-to-all-start.2 = ((bf16[8,4,6144]{2,1,0:T(4,128)(2,1)}), bf16[8,4,6144]{2,1,0:T(4,128)(2,1)}, u32[]{:S(2)}, u32[]{:S(2)}) async-start(bf16[8,4,6144]{2,1,0:T(4,128)(2,1)} %all_to_all.74), calls=%async_computation.2 | async-start | bytes 786432 | tf_op jit(solution)/shard_map/all_to_all | solution.py:90
  61.9 41.8 %all-to-all-start = ((bf16[8,4,6144]{2,1,0:T(4,128)(2,1)}), bf16[8,4,6144]{2,1,0:T(4,128)(2,1)}, u32[]{:S(2)}, u32[]{:S(2)}) async-start(bf16[8,4,6144]{2,1,0:T(4,128)(2,1)} %all_to_all.68), calls=%async_computation | async-start | bytes 786432 | tf_op jit(solution)/shard_map/all_to_all | solution.py:88
  103.7 67.2 %all-to-all-start.5 = ((bf16[4,8,2560]{2,0,1:T(4,128)(2,1)}), bf16[4,8,2560]{2,0,1:T(4,128)(2,1)}, u32[]{:S(2)}, u32[]{:S(2)}) async-start(bf16[4,8,2560]{2,0,1:T(4,128)(2,1)} %copy.76), calls=%async_computation.5 | async-start | bytes 327680 | tf_op jit(solution)/shard_map/all_to_all | solution.py:144
  170.8 15.8 %all-to-all-start.3 = ((bf16[4,8,6144]{2,0,1:T(4,128)(2,1)}), bf16[4,8,6144]{2,0,1:T(4,128)(2,1)S(1)}, u32[]{:S(2)}, u32[]{:S(2)}) async-start(bf16[4,8,6144]{2,0,1:T(4,128)(2,1)} %copy.71), calls=%async_computation.3 | async-start | bytes 786432 | tf_op jit(solution)/shard_map/all_to_all | solution.py:102
  176.8 2.9 %copy-start.7 = (f32[1024]{0:T(1024)S(1)}, f32[1024]{0:T(1024)}, u32[]{:S(2)}) copy-start(f32[1024]{0:T(1024)} %param.23) | copy-start | bytes 12292
  178.0 1.7 copy-start.4
  188.6 7.1 %copy-start.3 = (bf16[2,96,1024]{2,1,0:T(8,128)(2,1)S(1)}, bf16[2,96,1024]{2,1,0:T(8,128)(2,1)}, u32[]{:S(2)}) copy-start(bf16[2,96,1024]{2,1,0:T(8,128)(2,1)} %param.16) | copy-start | bytes 1179652
where the time goes:
time: 201 us; the launch traced here: 199 us
  local copies, waits for them, and re-layouts  74.7 us (37%)
  matrix products  37.3 us (19%)
  other arithmetic  36.8 us (18%)
  starting transfers between devices  33.5 us (17%)
  waiting for transfers between devices  14.4 us (7%)
    dot_general x12, matrix products, query_part(): jnp.dot(weights, values, preferred_element_type=jnp.float32)  15.2 us
    lt x20, other arithmetic, cand_part(): key_positions[None, :] < valid  12.7 us
    dynamic_slice x12, local copies, waits for them, and re-layouts, per_device(): lax.map(self_item, (heads_query, heads_keys, heads_values, item_valid))  8.53 us
    add x12, other arithmetic, query_part(): row_positions = first_row + jnp.arange(block_rows, dtype=jnp.int32)  8.29 us
    convert_element_type x3, local copies, waits for them, and re-layouts, per_device(): returned.astype(jnp.float32)  8.11 us
    dynamic_slice x12, local copies, waits for them, and re-layouts, self_item(): lax.map(query_part, (query.reshape(length // block_rows, block_rows, HD),...  7.94 us
    all_to_all x1, waiting for transfers between devices, per_device(): lax.all_to_all(to_items(keys), 'seq', split_axis=0, concat_axis=1, tiled=...  7.85 us
    squeeze x8, local copies, waits for them, and re-layouts, per_device(): lax.map(self_item, (heads_query, heads_keys, heads_values, item_valid))  7.62 us
  transfers between devices with their start and end apart: 6, of which 3 were waited for; matrix products, arithmetic and copies ran while one was open for 60% of the time, Pallas kernels for 0%

commit v1 on v0

--- a/solution.py
+++ b/solution.py
@@ -99,9 +99,30 @@
         jnp.where(item_hist[:, None] == members[None, :], lengths[None, :], 0), axis=1
     )
     attended = lax.map(self_item, (heads_query, heads_keys, heads_values, item_valid))
-    returned = lax.all_to_all(
-        attended.reshape(items_local, length * HD), "seq", split_axis=1, concat_axis=0, tiled=True
-    )
+
+    def mark_lane_for(sheet, dim_at, dim_k):
+        y = lax.axis_size("seq")
+        clean = lax.axis_index("seq")
+        x_next, before = (y, clean)
+        all_values = sheet.shape[dim_at] // x_next
+        kept_arr = list(sheet.shape)
+        kept_arr[dim_at] = all_values
+        r1 = kept_arr[dim_k]
+        kept_arr[dim_k] = r1 * x_next
+        a_next = jnp.zeros(kept_arr, sheet.dtype)
+        for j in range(x_next):
+            s_next = lax.dynamic_slice_in_dim(
+                sheet, (before ^ j) * all_values, all_values, axis=dim_at
+            )
+            if j:
+                by_rank = []
+                for k in range(x_next):
+                    by_rank.append((k, k ^ j))
+                s_next = lax.ppermute(s_next, "seq", by_rank)
+            a_next = lax.dynamic_update_slice_in_dim(a_next, s_next, (before ^ j) * r1, axis=dim_k)
+        return a_next
+
+    returned = mark_lane_for(attended.reshape(items_local, length * HD), 1, 0)
     returned = (
         returned.reshape(hist_local, H, tok_share, HD)
         .transpose(0, 2, 1, 3)

time: 201 us -> 224 us (1.11)
  local copies, waits for them, and re-layouts: 74.7 us -> 87 us
  waiting for transfers between devices: 14.4 us -> 19.4 us
  starting transfers between devices: 33.5 us -> 37.6 us
  other arithmetic: 36.8 us -> 39.6 us
    ppermute x0 -> x7, starting transfers between devices: none -> 12.6 us  [mark_lane_for(): s_next = lax.ppermute(s_next, 'seq', by_rank)]
    all_to_all x1, waiting for transfers between devices: 1.73 us -> 8.8 us  [per_device(): lax.all_to_all(to_items(values), 'seq', split_axis=0, concat_axis=1, tile...]
    dynamic_update_slice x0 -> x7, local copies, waits for them, and re-layouts: none -> 6.87 us  [mark_lane_for(): lax.dynamic_update_slice_in_dim(a_next, s_next, (before ^ j) * r1, axis=d...]
    all_to_all x1 -> x0, starting transfers between devices: 5.98 us -> none  [per_device(): lax.all_to_all(attended.reshape(items_local, length * HD), 'seq', split_a...]
    all_to_all x1 -> x0, waiting for transfers between devices: 4.8 us -> none  [per_device(): lax.all_to_all(attended.reshape(items_local, length * HD), 'seq', split_a...]
    all_to_all x2 -> x0, local copies, waits for them, and re-layouts: 2.82 us -> none  [per_device(): lax.all_to_all(attended.reshape(items_local, length * HD), 'seq', split_a...]
  transfers between devices with their start and end apart: 6 -> 12, of which waited for: 3 -> 4; matrix products, arithmetic and copies ran while one was open for 60% -> 36% of each run, Pallas kernels for 0% -> 0%
where the time goes in v1:
time: 224 us; the launch traced here: 222 us
  local copies, waits for them, and re-layouts  87 us (39%)
  other arithmetic  39.6 us (18%)
  starting transfers between devices  37.6 us (17%)
  matrix products  36.3 us (16%)
  waiting for transfers between devices  19.4 us (9%)
    dot_general x12, matrix products, query_part(): jnp.dot(weights, values, preferred_element_type=jnp.float32)  15.2 us
    lt x20, other arithmetic, cand_part(): key_positions[None, :] < valid  13.9 us
    ppermute x7, starting transfers between devices, mark_lane_for(): s_next = lax.ppermute(s_next, 'seq', by_rank)  12.6 us
    convert_element_type x3, local copies, waits for them, and re-layouts, per_device(): returned.astype(jnp.float32)  9.03 us
    dynamic_slice x12, local copies, waits for them, and re-layouts, per_device(): lax.map(self_item, (heads_query, heads_keys, heads_values, item_valid))  8.85 us
    all_to_all x1, waiting for transfers between devices, per_device(): lax.all_to_all(to_items(keys), 'seq', split_axis=0, concat_axis=1, tiled=...  8.84 us
    all_to_all x1, waiting for transfers between devices, per_device(): lax.all_to_all(to_items(values), 'seq', split_axis=0, concat_axis=1, tile...  8.8 us
    add x12, other arithmetic, query_part(): row_positions = first_row + jnp.arange(block_rows, dtype=jnp.int32)  8.1 us
  transfers between devices with their start and end apart: 12, of which 4 were waited for; matrix products, arithmetic and copies ran while one was open for 36% of the time, Pallas kernels for 0%

profile of v1, /device:TPU:0, one launch (start us, length us, event | category | flops | bytes accessed | tf_op | source)
XLA Modules:
  0.0 221.7 jit_solution(16595382955585027565)
XLA Ops:
  1.5 2.0 sort.31
  3.5 2.0 sort.32
  6.6 3.2 %fusion.37 = f32[64,2048]{1,0:T(8,128)S(1)} fusion(bf16[1024,4096]{1,0:T(8,128)(2,1)} %param.20, bf16[1,64,1024]{2,1,0:T(8,128)(2,1)} %param.17, f32[1024]{0:T(1024)} %param.22, f32[64]{0:T(128)S(1)} %add_rsqrt_fusion.3), kind=kOutput, calls=%fused_computation.50 | convolution fusion | flops 268697600 | bytes 4854016 | tf_op jit(solution)/shard_map/dot_general | solution.py:144
  13.5 7.3 %all-to-all-start.3 = ((bf16[8,4,2560]{2,1,0:T(4,128)(2,1)}), bf16[8,4,2560]{2,1,0:T(4,128)(2,1)}, u32[]{:S(2)}, u32[]{:S(2)}) async-start(bf16[8,4,2560]{2,1,0:T(4,128)(2,1)} %all_to_all.67), calls=%async_computation.3 | async-start | bytes 327680 | tf_op jit(solution)/shard_map/all_to_all | solution.py:162
  21.2 6.8 %fusion.61 = (bf16[192,4096]{1,0:T(8,128)(2,1)S(1)}, f32[192,4096]{1,0:T(8,128)}) fusion(bf16[192,1024]{1,0:T(8,128)(2,1)S(1)} %bitcast.137, bf16[1024,4096]{1,0:T(8,128)(2,1)} %param.20), kind=kOutput, calls=%fused_computation.126 | convolution fusion | flops 1611399168 | bytes 13500416 | tf_op jit(solution)/shard_map/dot_general | solution.py:74
  30.1 1.3 all_to_all.61
  31.4 6.0 %all-to-all-start.1 = ((bf16[8,4,6144]{2,1,0:T(4,128)(2,1)}), bf16[8,4,6144]{2,1,0:T(4,128)(2,1)}, u32[]{:S(2)}, u32[]{:S(2)}) async-start(bf16[8,4,6144]{2,1,0:T(4,128)(2,1)} %all_to_all.61), calls=%async_computation.1 | async-start | bytes 786432 | tf_op jit(solution)/shard_map/all_to_all | solution.py:89
  38.5 1.3 all_to_all.64
  39.7 8.8 %all-to-all-done.1 = bf16[8,4,6144]{2,1,0:T(4,128)(2,1)} async-done(((bf16[8,4,6144]{2,1,0:T(4,128)(2,1)}), bf16[8,4,6144]{2,1,0:T(4,128)(2,1)}, u32[]{:S(2)}, u32[]{:S(2)}) %all-to-all-start.1) | async-done | bytes 393248 | tf_op jit(solution)/shard_map/all_to_all | solution.py:89
  48.6 4.1 %all-to-all-start.2 = ((bf16[8,4,6144]{2,1,0:T(4,128)(2,1)}), bf16[8,4,6144]{2,1,0:T(4,128)(2,1)}, u32[]{:S(2)}, u32[]{:S(2)}) async-start(bf16[8,4,6144]{2,1,0:T(4,128)(2,1)} %all_to_all.64), calls=%async_computation.2 | async-start | bytes 786432 | tf_op jit(solution)/shard_map/all_to_all | solution.py:90
  53.8 1.3 all_to_all.58
  55.1 8.8 %all-to-all-done.2 = bf16[8,4,6144]{2,1,0:T(4,128)(2,1)} async-done(((bf16[8,4,6144]{2,1,0:T(4,128)(2,1)}), bf16[8,4,6144]{2,1,0:T(4,128)(2,1)}, u32[]{:S(2)}, u32[]{:S(2)}) %all-to-all-start.2) | async-done | bytes 393248 | tf_op jit(solution)/shard_map/all_to_all | solution.py:90
  63.9 3.6 %all-to-all-start = ((bf16[8,4,6144]{2,1,0:T(4,128)(2,1)}), bf16[8,4,6144]{2,1,0:T(4,128)(2,1)S(1)}, u32[]{:S(2)}, u32[]{:S(2)}) async-start(bf16[8,4,6144]{2,1,0:T(4,128)(2,1)} %all_to_all.58), calls=%async_computation | async-start | bytes 786432 | tf_op jit(solution)/shard_map/all_to_all | solution.py:88
  69.7 2.0 copy.64
  71.7 1.7 reshape.184
  73.4 2.0 copy.67
  75.4 2.6 %reshape.186 = bf16[4,768,64]{2,1,0:T(8,128)(2,1)} reshape(bf16[4,8,6144]{2,1,0:T(8,128)(2,1)} %copy.67) | data formatting | bytes 786432 | tf_op jit(solution)/shard_map/reshape | solution.py:94
  80.0 2.6 %reshape.182 = bf16[4,768,64]{2,1,0:T(8,128)(2,1)} reshape(bf16[4,8,6144]{2,1,0:T(8,128)(2,1)} %copy.61) | data formatting | bytes 786432 | tf_op jit(solution)/shard_map/reshape | solution.py:92
  82.6 55.9 %while.44 = (s32[]{:T(128)}, bf16[4,768,64]{2,1,0:T(8,128)(2,1)}, bf16[4,768,64]{2,1,0:T(8,128)(2,1)}, bf16[4,768,64]{2,1,0:T(8,128)(2,1)S(1)}, s32[4]{0:T(128)S...) while((s32[]{:T(128)}, bf16[4,768,64]{2,1,0:T(8,128)(2,1)}, ...), condition=%wide.region_5.6_spmd, body=%wide.region_2.5_spmd.sunk | while | flops 52118532 | bytes 1578542 | solution.py:101
  85.1 9.7 %while.47 = (s32[]{:T(128)}, bf16[3,256,64]{1,2,0:T(8,128)(2,1)}, s32[3]{0:T(128)S(1)}, s32[]{:T(128)}, bf16[3,256,64]{2,1,0:T(8,128)(2,1)S(1)}, /*index=5*/bf16...) while((s32[]{:T(128)}, bf16[3,256,64]{1,2,0:T(8,128)(2,1)}, ...), condition=%wide.region_4.4_spmd.clone.clone, body=%wide.region_3.3_spmd.clone.clone.sunk | while | flops 52118528 | bytes 496489 | solution.py:34
  87.1 1.3 fusion.85
  90.4 1.3 fusion.85
  93.6 1.3 fusion.85
  94.8 1.1 copy.79
  99.1 9.7 %while.47 = (s32[]{:T(128)}, bf16[3,256,64]{1,2,0:T(8,128)(2,1)}, s32[3]{0:T(128)S(1)}, s32[]{:T(128)}, bf16[3,256,64]{2,1,0:T(8,128)(2,1)S(1)}, /*index=5*/bf16...) while((s32[]{:T(128)}, bf16[3,256,64]{1,2,0:T(8,128)(2,1)}, ...), condition=%wide.region_4.4_spmd.clone.clone, body=%wide.region_3.3_spmd.clone.clone.sunk | while | flops 52118528 | bytes 496489 | solution.py:34
  101.1 1.3 fusion.85
  104.3 1.3 fusion.85
  107.6 1.3 fusion.85
  108.8 1.1 copy.79
  113.1 9.7 %while.47 = (s32[]{:T(128)}, bf16[3,256,64]{1,2,0:T(8,128)(2,1)}, s32[3]{0:T(128)S(1)}, s32[]{:T(128)}, bf16[3,256,64]{2,1,0:T(8,128)(2,1)S(1)}, /*index=5*/bf16...) while((s32[]{:T(128)}, bf16[3,256,64]{1,2,0:T(8,128)(2,1)}, ...), condition=%wide.region_4.4_spmd.clone.clone, body=%wide.region_3.3_spmd.clone.clone.sunk | while | flops 52118528 | bytes 496489 | solution.py:34
  115.1 1.3 fusion.85
  118.3 1.3 fusion.85
  121.5 1.3 fusion.85
  122.8 1.1 copy.79
  127.1 9.7 %while.47 = (s32[]{:T(128)}, bf16[3,256,64]{1,2,0:T(8,128)(2,1)}, s32[3]{0:T(128)S(1)}, s32[]{:T(128)}, bf16[3,256,64]{2,1,0:T(8,128)(2,1)S(1)}, /*index=5*/bf16...) while((s32[]{:T(128)}, bf16[3,256,64]{1,2,0:T(8,128)(2,1)}, ...), condition=%wide.region_4.4_spmd.clone.clone, body=%wide.region_3.3_spmd.clone.clone.sunk | while | flops 52118528 | bytes 496489 | solution.py:34
  129.0 1.3 fusion.85
  132.3 1.3 fusion.85
  135.5 1.3 fusion.85
  136.8 1.1 copy.79
  138.6 1.7 reshape.187
  141.8 1.4 collective-permute-start
  144.2 1.1 collective-permute-start.2
  145.3 1.8 collective-permute-start.3
  147.1 2.0 collective-permute-start.4
  149.1 34.2 %while.46 = (s32[]{:T(128)}, bf16[4,320,64]{2,1,0:T(8,128)(2,1)}, bf16[4,320,64]{2,1,0:T(8,128)(2,1)}, bf16[4,768,64]{2,1,0:T(8,128)(2,1)S(1)}, s32[4]{0:T(128)S...) while((s32[]{:T(128)}, bf16[4,320,64]{2,1,0:T(8,128)(2,1)}, ...), condition=%wide.region_12.13_spmd, body=%wide.region_9.12_spmd.sunk | while | flops 12931844 | bytes 1027586 | solution.py:164
  151.6 5.4 %while.48 = (s32[]{:T(128)}, bf16[5,64,64]{2,1,0:T(8,128)(2,1)S(1)}, s32[]{:T(128)}, bf16[5,64,64]{2,1,0:T(8,128)(2,1)S(1)}, bf16[768,64]{1,0:T(8,128)(2,1)S(1)}, /*index=5*/bf16[768,64]{1,0:T(8,128)(2,1)S(1)}, s32[]{:T(128)}) while((s32[]{:T(128)}, bf16[5,64,64]{2,1,0:T(8,128)(2,1)S(1)}, s32[]{:T(128)}, ...), condition=%wide.region_11.11_spmd.clone, body=%wide.region_10.10_spmd.clone.sunk | while | flops 12931842 | bytes 428881 | solution.py:52
  160.2 5.4 %while.48 = (s32[]{:T(128)}, bf16[5,64,64]{2,1,0:T(8,128)(2,1)S(1)}, s32[]{:T(128)}, bf16[5,64,64]{2,1,0:T(8,128)(2,1)S(1)}, bf16[768,64]{1,0:T(8,128)(2,1)S(1)}, /*index=5*/bf16[768,64]{1,0:T(8,128)(2,1)S(1)}, s32[]{:T(128)}) while((s32[]{:T(128)}, bf16[5,64,64]{2,1,0:T(8,128)(2,1)S(1)}, s32[]{:T(128)}, ...), condition=%wide.region_11.11_spmd.clone, body=%wide.region_10.10_spmd.clone.sunk | while | flops 12931842 | bytes 428881 | solution.py:52
  168.7 5.4 %while.48 = (s32[]{:T(128)}, bf16[5,64,64]{2,1,0:T(8,128)(2,1)S(1)}, s32[]{:T(128)}, bf16[5,64,64]{2,1,0:T(8,128)(2,1)S(1)}, bf16[768,64]{1,0:T(8,128)(2,1)S(1)}, /*index=5*/bf16[768,64]{1,0:T(8,128)(2,1)S(1)}, s32[]{:T(128)}) while((s32[]{:T(128)}, bf16[5,64,64]{2,1,0:T(8,128)(2,1)S(1)}, s32[]{:T(128)}, ...), condition=%wide.region_11.11_spmd.clone, body=%wide.region_10.10_spmd.clone.sunk | while | flops 12931842 | bytes 428881 | solution.py:52
  177.3 5.4 %while.48 = (s32[]{:T(128)}, bf16[5,64,64]{2,1,0:T(8,128)(2,1)S(1)}, s32[]{:T(128)}, bf16[5,64,64]{2,1,0:T(8,128)(2,1)S(1)}, bf16[768,64]{1,0:T(8,128)(2,1)S(1)}, /*index=5*/bf16[768,64]{1,0:T(8,128)(2,1)S(1)}, s32[]{:T(128)}) while((s32[]{:T(128)}, bf16[5,64,64]{2,1,0:T(8,128)(2,1)S(1)}, s32[]{:T(128)}, ...), condition=%wide.region_11.11_spmd.clone, body=%wide.region_10.10_spmd.clone.sunk | while | flops 12931842 | bytes 428881 | solution.py:52
  183.3 1.2 all_to_all.70
  185.3 4.0 %all-to-all-start.4 = ((bf16[4,8,2560]{2,0,1:T(4,128)(2,1)}), bf16[4,8,2560]{2,0,1:T(4,128)(2,1)S(1)}, u32[]{:S(2)}, u32[]{:S(2)}) async-start(bf16[4,8,2560]{2,0,1:T(4,128)(2,1)} %copy.72), calls=%async_computation.4 | async-start | bytes 327680 | tf_op jit(solution)/shard_map/all_to_all | solution.py:165
  189.3 3.8 %collective-permute-start.5 = (bf16[4,6144]{1,0:T(4,128)(2,1)}, bf16[4,6144]{1,0:T(4,128)(2,1)S(1)}, u32[]{:S(2)}, u32[]{:S(2)}) collective-permute-start(bf16[4,6144]{1,0:T(4,128)(2,1)} %get-tuple-element.264), channel_id=1, source_target_pairs={{0,6},{1,7},{2,4},{3,5},{4,2},{5,3},{6,0},{7,1},{8,14},{9,15},{10,... | collective-permute-start | bytes 147464 | tf_op jit(solution)/shard_map/ppermute | solution.py:121
  193.1 1.4 constant_dynamic-update-slice_fusion.6
  194.5 1.5 collective-permute-start.6
  196.0 1.4 constant_dynamic-update-slice_fusion.5
  197.4 1.4 constant_dynamic-update-slice_fusion.4
  202.2 2.9 %reshape.195 = f32[2,16,96,64]{3,2,1,0:T(8,128)} reshape(bf16[32,6144]{1,0:T(8,128)(2,1)} %constant_dynamic-update-slice_fusion) | data formatting | bytes 1179648 | tf_op jit(solution)/shard_map/convert_element_type | solution.py:132
  205.1 1.0 convert_multiply_fusion.2
  206.1 3.5 %copy.74 = f32[2,96,16,64]{3,2,1,0:T(8,128)} copy(f32[2,96,16,64]{3,1,2,0:T(8,128)} %bitcast.134) | data formatting | bytes 1572864 | tf_op jit(solution)/shard_map/convert_element_type | solution.py:132
  209.6 2.7 %reshape.223 = f32[192,1024]{1,0:T(8,128)} reshape(f32[2,96,16,64]{3,2,1,0:T(8,128)} %copy.74) | data formatting | bytes 1572864 | tf_op jit(solution)/shard_map/convert_element_type | solution.py:132
  212.3 1.8 mul.187
  214.0 1.6 reduce_sum.47
  215.8 2.8 %fusion.39 = bf16[192,1024]{1,0:T(8,128)(2,1)} fusion(bf16[1024,1024]{1,0:T(8,128)(2,1)S(1)} %copy-done, f32[192,1024]{1,0:T(8,128)} %reshape.223, f32[192,4096]{1,0:T(8,128)} %get-tuple-element.276, f32[1024]{0:T(1024)S(1)} %copy-done.10, f32[192]{0:T(256)S(1)} %rsqrt.37, bf16[192,1024]{1,0:T(8,128)(2,1)S(1)} %bitcast.143), kind=kOutput, calls=%fused_computation.53 | convolution fusion | flops 405209088 | bytes 4461312 | tf_op jit(solution)/shard_map/dot_general | solution.py:134
  220.5 1.2 fusion.41
  (210 shorter events, 92.6 us)
Async XLA Ops:
  0.6 215.1 %copy-start = (bf16[1024,1024]{1,0:T(8,128)(2,1)S(1)}, bf16[1024,1024]{1,0:T(8,128)(2,1)}, u32[]{:S(2)}) copy-start(bf16[1024,1024]{1,0:T(8,128)(2,1)} %param.21) | copy-start | bytes 6291460
  6.6 4.9 %copy-start.1 = (s32[1,64]{1,0:T(1,128)S(1)}, s32[1,64]{1,0:T(1,128)}, u32[]{:S(2)}) copy-start(s32[1,64]{1,0:T(1,128)} %param.19) | copy-start | bytes 772
  9.8 0.8 copy-start.7
  10.6 10.2 %copy-start.4 = (bf16[2,96,1024]{2,1,0:T(8,128)(2,1)S(1)}, bf16[2,96,1024]{2,1,0:T(8,128)(2,1)}, u32[]{:S(2)}) copy-start(bf16[2,96,1024]{2,1,0:T(8,128)(2,1)} %param.16) | copy-start | bytes 1179652
  10.8 10.2 %copy-start.9 = (f32[1024]{0:T(1024)S(1)}, f32[1024]{0:T(1024)}, u32[]{:S(2)}) copy-start(f32[1024]{0:T(1024)} %param.22) | copy-start | bytes 12292
  13.5 17.8 %all-to-all-start.3 = ((bf16[8,4,2560]{2,1,0:T(4,128)(2,1)}), bf16[8,4,2560]{2,1,0:T(4,128)(2,1)}, u32[]{:S(2)}, u32[]{:S(2)}) async-start(bf16[8,4,2560]{2,1,0:T(4,128)(2,1)} %all_to_all.67), calls=%async_computation.3 | async-start | bytes 327680 | tf_op jit(solution)/shard_map/all_to_all | solution.py:162
  30.1 7.3 %copy-start.3 = (bf16[192,1024]{1,0:T(8,128)(2,1)S(1)}, bf16[192,1024]{1,0:T(8,128)(2,1)}, u32[]{:S(2)}) copy-start(bf16[192,1024]{1,0:T(8,128)(2,1)} %get-tuple-element.258) | copy-start | bytes 1179652
  31.4 17.2 %all-to-all-start.1 = ((bf16[8,4,6144]{2,1,0:T(4,128)(2,1)}), bf16[8,4,6144]{2,1,0:T(4,128)(2,1)}, u32[]{:S(2)}, u32[]{:S(2)}) async-start(bf16[8,4,6144]{2,1,0:T(4,128)(2,1)} %all_to_all.61), calls=%async_computation.1 | async-start | bytes 786432 | tf_op jit(solution)/shard_map/all_to_all | solution.py:89
  38.4 14.2 %copy-start.2 = (bf16[192,1024]{1,0:T(8,128)(2,1)S(1)}, bf16[192,1024]{1,0:T(8,128)(2,1)}, u32[]{:S(2)}) copy-start(bf16[192,1024]{1,0:T(8,128)(2,1)} %get-tuple-element.260) | copy-start | bytes 1179652
  48.6 15.3 %all-to-all-start.2 = ((bf16[8,4,6144]{2,1,0:T(4,128)(2,1)}), bf16[8,4,6144]{2,1,0:T(4,128)(2,1)}, u32[]{:S(2)}, u32[]{:S(2)}) async-start(bf16[8,4,6144]{2,1,0:T(4,128)(2,1)} %all_to_all.64), calls=%async_computation.2 | async-start | bytes 786432 | tf_op jit(solution)/shard_map/all_to_all | solution.py:90
  52.9 14.8 %copy-start.11 = (s32[2]{0:T(128)S(1)}, s32[2]{0:T(128)}, u32[]{:S(2)}) copy-start(s32[2]{0:T(128)} %param.18) | copy-start | bytes 28
  63.9 15.2 %all-to-all-start = ((bf16[8,4,6144]{2,1,0:T(4,128)(2,1)}), bf16[8,4,6144]{2,1,0:T(4,128)(2,1)S(1)}, u32[]{:S(2)}, u32[]{:S(2)}) async-start(bf16[8,4,6144]{2,1,0:T(4,128)(2,1)} %all_to_all.58), calls=%async_computation | async-start | bytes 786432 | tf_op jit(solution)/shard_map/all_to_all | solution.py:88
  141.8 47.4 %collective-permute-start = (bf16[4,6144]{1,0:T(4,128)(2,1)}, bf16[4,6144]{1,0:T(4,128)(2,1)}, u32[]{:S(2)}, u32[]{:S(2)}) collective-permute-start(bf16[4,6144]{1,0:T(4,128)(2,1)} %get-tuple-element.269), channel_id=1, source_target_pairs={{0,1},{1,0},{2,3},{3,2},{4,5},{5,4},{6,7},{7,6},{8,9},{9,8},{10,11... | collective-permute-start | bytes 147464 | tf_op jit(solution)/shard_map/ppermute | solution.py:121
  143.3 51.3 %collective-permute-start.1 = (bf16[4,6144]{1,0:T(4,128)(2,1)}, bf16[4,6144]{1,0:T(4,128)(2,1)}, u32[]{:S(2)}, u32[]{:S(2)}) collective-permute-start(bf16[4,6144]{1,0:T(4,128)(2,1)} %get-tuple-element.268), channel_id=1, source_target_pairs={{0,2},{1,3},{2,0},{3,1},{4,6},{5,7},{6,4},{7,5},{8,10},{9,11},{10,... | collective-permute-start | bytes 147464 | tf_op jit(solution)/shard_map/ppermute | solution.py:121
  144.2 53.3 %collective-permute-start.2 = (bf16[4,6144]{1,0:T(4,128)(2,1)}, bf16[4,6144]{1,0:T(4,128)(2,1)}, u32[]{:S(2)}, u32[]{:S(2)}) collective-permute-start(bf16[4,6144]{1,0:T(4,128)(2,1)} %get-tuple-element.267), channel_id=1, source_target_pairs={{0,3},{1,2},{2,1},{3,0},{4,7},{5,6},{6,5},{7,4},{8,11},{9,10},{10,... | collective-permute-start | bytes 147464 | tf_op jit(solution)/shard_map/ppermute | solution.py:121
  145.3 53.6 %collective-permute-start.3 = (bf16[4,6144]{1,0:T(4,128)(2,1)}, bf16[4,6144]{1,0:T(4,128)(2,1)S(1)}, u32[]{:S(2)}, u32[]{:S(2)}) collective-permute-start(bf16[4,6144]{1,0:T(4,128)(2,1)} %get-tuple-element.266), channel_id=1, source_target_pairs={{0,4},{1,5},{2,6},{3,7},{4,0},{5,1},{6,2},{7,3},{8,12},{9,13},{10,... | collective-permute-start | bytes 147464 | tf_op jit(solution)/shard_map/ppermute | solution.py:121
  147.1 52.4 %collective-permute-start.4 = (bf16[4,6144]{1,0:T(4,128)(2,1)}, bf16[4,6144]{1,0:T(4,128)(2,1)S(1)}, u32[]{:S(2)}, u32[]{:S(2)}) collective-permute-start(bf16[4,6144]{1,0:T(4,128)(2,1)} %get-tuple-element.265), channel_id=1, source_target_pairs={{0,5},{1,4},{2,7},{3,6},{4,1},{5,0},{6,3},{7,2},{8,13},{9,12},{10,... | collective-permute-start | bytes 147464 | tf_op jit(solution)/shard_map/ppermute | solution.py:121
  185.3 33.3 %all-to-all-start.4 = ((bf16[4,8,2560]{2,0,1:T(4,128)(2,1)}), bf16[4,8,2560]{2,0,1:T(4,128)(2,1)S(1)}, u32[]{:S(2)}, u32[]{:S(2)}) async-start(bf16[4,8,2560]{2,0,1:T(4,128)(2,1)} %copy.72), calls=%async_computation.4 | async-start | bytes 327680 | tf_op jit(solution)/shard_map/all_to_all | solution.py:165
  189.3 10.9 %collective-permute-start.5 = (bf16[4,6144]{1,0:T(4,128)(2,1)}, bf16[4,6144]{1,0:T(4,128)(2,1)S(1)}, u32[]{:S(2)}, u32[]{:S(2)}) collective-permute-start(bf16[4,6144]{1,0:T(4,128)(2,1)} %get-tuple-element.264), channel_id=1, source_target_pairs={{0,6},{1,7},{2,4},{3,5},{4,2},{5,3},{6,0},{7,1},{8,14},{9,15},{10,... | collective-permute-start | bytes 147464 | tf_op jit(solution)/shard_map/ppermute | solution.py:121
  194.5 7.0 %collective-permute-start.6 = (bf16[4,6144]{1,0:T(4,128)(2,1)}, bf16[4,6144]{1,0:T(4,128)(2,1)S(1)}, u32[]{:S(2)}, u32[]{:S(2)}) collective-permute-start(bf16[4,6144]{1,0:T(4,128)(2,1)} %get-tuple-element.263), channel_id=1, source_target_pairs={{0,7},{1,6},{2,5},{3,4},{4,3},{5,2},{6,1},{7,0},{8,15},{9,14},{10,... | collective-permute-start | bytes 147464 | tf_op jit(solution)/shard_map/ppermute | solution.py:121
  212.3 3.5 %copy-start.5 = (bf16[2,96,1024]{2,1,0:T(8,128)(2,1)S(1)}, bf16[2,96,1024]{2,1,0:T(8,128)(2,1)}, u32[]{:S(2)}) copy-start(bf16[2,96,1024]{2,1,0:T(8,128)(2,1)} %param.16) | copy-start | bytes 1179652
  212.3 3.5 %copy-start.10 = (f32[1024]{0:T(1024)S(1)}, f32[1024]{0:T(1024)}, u32[]{:S(2)}) copy-start(f32[1024]{0:T(1024)} %param.23) | copy-start | bytes 12292
  219.0 1.5 copy-start.6
  219.0 1.5 copy-start.8
